TPU v7x, 32 devices: a whole 2x2x4 slice. The times are simulated.
32 devices in a mesh: py: 4 (over y, core), pz: 8 (over z, x).
Axes of the slice: x: 2, y: 2, z: 4, core: 2. Of those that a mesh axis runs over, the one named last changes fastest.
Arguments:
- wavefunctions: float32 [2, 8, 128, 128, 128], P(None, None, 'pz', 'py'), may hold values from -6 to 6
- potential: float32 [128, 128, 128], P('pz', 'py'), may hold values from -4 to 4
- cutoff_sq: int32 [1], replicated, may hold values from 2304 to 4096
- locked_mask: int32 [8], replicated, may hold values 0 or 1
Outputs:
- applied: float32 [2, 8, 128, 128, 128], P(None, None, 'pz', 'py')
- rayleigh: float32 [8], replicated
- residual_norm: float32 [8], replicated
All inputs are finite; a program needn't handle non-finite values.
Results may differ from a plain program's by a relative error of at most 0.00005.
Values sent between devices are 32-bit elements; how exact they have to be, the bound alone decides.
A program may use at most 64 MiB of HBM per device.

v0:
```python
import math
import jax
import jax.numpy as jnp
from jax import lax
from jax.sharding import PartitionSpec as P


def make_tables(length, inverse):
    counter = jnp.arange(length, dtype=jnp.int32)
    phase = counter[:, None] * counter[None, :] % length
    angle = 2.0 * math.pi / length * phase.astype(jnp.float32)
    if inverse:
        return (jnp.cos(angle) / length, jnp.sin(angle) / length)
    return (jnp.cos(angle), -jnp.sin(angle))


def transform_axis(field, axis, tables):
    cosines, sines = tables
    letters = "abcdefgh"[: field.ndim - 1]
    place = axis - 1
    source = letters[:place] + "n" + letters[place + 1 :]
    target = letters[:place] + "k" + letters[place + 1 :]
    form = source + ",kn->" + target
    real_part = field[0]
    imag_part = field[1]
    high = lax.Precision.HIGHEST
    out_real = jnp.einsum(form, real_part, cosines, precision=high) - jnp.einsum(
        form, imag_part, sines, precision=high
    )
    out_imag = jnp.einsum(form, real_part, sines, precision=high) + jnp.einsum(
        form, imag_part, cosines, precision=high
    )
    return jnp.stack([out_real, out_imag])


def signed_square(counter, length):
    signed = jnp.where(counter < length // 2, counter, counter - length)
    return signed * signed


def kinetic_table(first_sq, second_sq, third_sq, cutoff_sq, length):
    total = first_sq[:, None, None] + second_sq[None, :, None] + third_sq[None, None, :]
    keep = (total <= cutoff_sq[0]).astype(jnp.float32)
    return 0.5 * (math.pi / length) ** 2 * total.astype(jnp.float32) * keep


def slab_kinetic(field, cutoff_sq, forward, inverse):
    parts, bands, rows_z, rows_y, length = field.shape
    size_y = lax.axis_size("py")
    size_z = lax.axis_size("pz")
    along_x = transform_axis(field, 4, forward)
    flat = jnp.moveaxis(along_x, 1, 3).reshape(parts, rows_z, rows_y, bands * length)
    planes = lax.all_to_all(
        lax.all_to_all(flat, "py", split_axis=3, concat_axis=2, tiled=True),
        "pz",
        split_axis=3,
        concat_axis=1,
        tiled=True,
    )
    width = planes.shape[3]
    start = lax.axis_index("py") * (bands * length // size_y) + lax.axis_index("pz") * width
    column = start + jnp.arange(width, dtype=jnp.int32)
    full_counter = jnp.arange(length, dtype=jnp.int32)
    full_sq = signed_square(full_counter, length)
    kinetic = kinetic_table(
        full_sq, full_sq, signed_square(column % length, length), cutoff_sq, length
    )
    spectrum = transform_axis(transform_axis(planes, 1, forward), 2, forward) * kinetic
    spatial = transform_axis(transform_axis(spectrum, 2, inverse), 1, inverse)
    returned = lax.all_to_all(
        lax.all_to_all(spatial, "py", split_axis=2, concat_axis=3, tiled=True),
        "pz",
        split_axis=1,
        concat_axis=3,
        tiled=True,
    )
    ordered = returned.reshape(parts, rows_z, rows_y, size_z, size_y, width)
    ordered = jnp.swapaxes(ordered, 3, 4).reshape(parts, rows_z, rows_y, bands, length)
    return transform_axis(jnp.moveaxis(ordered, 3, 1), 4, inverse)


def apply_kinetic(field, cutoff_sq, forward, inverse):
    return slab_kinetic(field, cutoff_sq, forward, inverse)


def body(wavefunctions, potential, cutoff_sq, locked_mask):
    length = wavefunctions.shape[4]
    forward = make_tables(length, False)
    inverse = make_tables(length, True)
    blocks = wavefunctions.shape[1] // 4

    def one_block(block, result):
        piece = lax.dynamic_slice_in_dim(wavefunctions, block * 4, 4, 1)
        done = apply_kinetic(piece, cutoff_sq, forward, inverse)
        return lax.dynamic_update_slice_in_dim(result, done, block * 4, 1)

    kinetic_part = lax.fori_loop(0, blocks, one_block, jnp.zeros_like(wavefunctions))
    applied = kinetic_part + potential[None, None] * wavefunctions
    norm_local = jnp.sum(wavefunctions * wavefunctions, axis=(0, 2, 3, 4))
    correlation_local = jnp.sum(wavefunctions * applied, axis=(0, 2, 3, 4))
    norm_sq, correlation = lax.psum((norm_local, correlation_local), ("py", "pz"))
    rayleigh = correlation / norm_sq
    residual = applied - rayleigh[None, :, None, None, None] * wavefunctions
    residual_sq = lax.psum(jnp.sum(residual * residual, axis=(0, 2, 3, 4)), ("py", "pz"))
    residual_norm = jnp.sqrt(residual_sq / norm_sq) * (1.0 - locked_mask.astype(jnp.float32))
    return (applied, rayleigh, residual_norm)


def solution(mesh):
    in_specs = (P(None, None, "pz", "py", None), P("pz", "py", None), P(), P())
    out_specs = (P(None, None, "pz", "py", None), P(), P())
    return jax.shard_map(body, mesh=mesh, in_specs=in_specs, out_specs=out_specs, check_vma=False)
```

profile of v0, /device:TPU:0, one launch (start us, length us, event | category | flops | bytes accessed | tf_op | source)
XLA Modules:
  0.0 693.6 jit_solution(16688748125790381216)
XLA Ops:
  3.2 599.9 %while.18 = (s32[]{:T(128)}, f32[2,8,16,32,128]{4,3,2,1,0:T(8,128)}, f32[2,8,16,32,128]{4,3,2,1,0:T(8,128)}, s32[1]{0:T(128)}, s32[]{:T(128)}, /*index=5*/s32[]{...) while((s32[]{:T(128)}, ...), condition=%wide.region_1.2_spmd.clone.clone, body=%wide.region_0.1_spmd.clone.clone.sunk | while | flops 9676570624 | bytes 232916592 | solution.py:97
  13.3 7.5 %copy.142 = f32[2,16,32,4,128]{2,1,0,4,3:T(8,128)} copy(f32[2,16,32,4,128]{4,2,1,3,0:T(8,128)S(1)} %maximum_bitcast_fusion.2) | data formatting | bytes 4194304 | tf_op jit(solution)/shard_map/while/body/eval_jaxpr/reshape | solution.py:52
  20.7 6.1 reshape.143
  26.9 30.2 %all_to_all.204 = f32[4,1,131072]{2,1,0:T(1,128)} all-to-all(f32[4,1,131072]{2,1,0:T(1,128)S(1)} %reshape.143), channel_id=1, replica_groups=mesh['py'=4,'pz'=8] {'py'}, dimensions={0} | all-to-all | bytes 4194304 | tf_op jit(solution)/shard_map/while/body/eval_jaxpr/all_to_all | solution.py:54
  57.6 7.7 %reduce.4 = f32[4,131072]{1,0:T(4,128)S(1)} reduce(f32[4,1,131072]{2,1,0:T(1,128)} %all_to_all.204, f32[]{:T(128)} %broadcast.656), dimensions={1}, to_apply=%all_to_all.178.reduce_sub_computation | reduce | bytes 4194308 | tf_op jit(solution)/shard_map/while/body/eval_jaxpr/all_to_all | solution.py:54
  65.3 6.1 reshape.144
  71.4 5.2 copy.143
  81.3 6.9 all-to-all-start.1
  89.3 46.3 %all-to-all-done.1 = f32[2,16,128,128]{2,1,0,3:T(8,128)S(1)} async-done(((f32[2,16,128,128]{2,1,0,3:T(8,128)}), f32[2,16,128,128]{2,1,0,3:T(8,128)S(1)}, u32[]{:S(2)}, u32[]{:S(2)}) %all-to-all-start.1) | async-done | bytes 2097184 | tf_op jit(solution)/shard_map/while/body/eval_jaxpr/all_to_all | solution.py:53
  170.9 28.1 %all_to_all.205 = f32[2,128,128,16]{1,3,0,2:T(8,128)S(1)} all-to-all(f32[2,128,128,16]{1,3,0,2:T(8,128)S(1)} %copy.151), channel_id=1, replica_groups=mesh['py'=4,'pz'=8] {'py'}, dimensions={2} | all-to-all | bytes 4194304 | tf_op jit(solution)/shard_map/while/body/eval_jaxpr/all_to_all | solution.py:71
  203.8 7.2 %reshape.145 = f32[8,1,65536]{2,1,0:T(1,128)} reshape(f32[128,2,32,64]{3,2,1,0:T(8,128)} %bitcast.327) | data formatting | bytes 4194304 | tf_op jit(solution)/shard_map/while
  214.9 48.0 %all-to-all-done.3 = f32[8,1,65536]{2,1,0:T(1,128)S(1)} async-done(((f32[8,1,65536]{2,1,0:T(1,128)}), f32[8,1,65536]{2,1,0:T(1,128)S(1)}, u32[]{:S(2)}, u32[]{:S(2)}) %all-to-all-start.3) | async-done | bytes 2097184 | tf_op jit(solution)/shard_map/while/body/eval_jaxpr/all_to_all | solution.py:70
  264.8 7.2 %reduce.5 = f32[8,65536]{1,0:T(8,128)S(1)} reduce(f32[8,1,65536]{2,1,0:T(1,128)} %copy-done, f32[]{:T(128)} %broadcast.657), dimensions={1}, to_apply=%all_to_all.189.reduce_sub_computation | reduce | bytes 4194308 | tf_op jit(solution)/shard_map/while/body/eval_jaxpr/all_to_all | solution.py:70
  275.6 7.0 %copy.154 = f32[2,16,32,8,64]{2,4,3,1,0:T(8,128)} copy(f32[2,16,32,8,64]{4,2,0,1,3:T(8,128)} %bitcast.326) | data formatting | bytes 4194304 | tf_op jit(solution)/shard_map/while/body/eval_jaxpr/all_to_all | solution.py:70
  282.6 7.9 %copy.155 = f32[2,16,32,4,8,16]{2,5,4,3,1,0:T(8,128)} copy(f32[2,16,32,4,8,16]{2,5,3,4,1,0:T(8,128)} %bitcast.320) | data formatting | bytes 4194304 | tf_op jit(solution)/shard_map/while/body/eval_jaxpr/transpose | solution.py:78
  290.5 5.6 copy.156
  313.5 7.5 %copy.142 = f32[2,16,32,4,128]{2,1,0,4,3:T(8,128)} copy(f32[2,16,32,4,128]{4,2,1,3,0:T(8,128)S(1)} %maximum_bitcast_fusion.2) | data formatting | bytes 4194304 | tf_op jit(solution)/shard_map/while/body/eval_jaxpr/reshape | solution.py:52
  321.0 6.1 reshape.143
  327.2 29.1 %all_to_all.204 = f32[4,1,131072]{2,1,0:T(1,128)} all-to-all(f32[4,1,131072]{2,1,0:T(1,128)S(1)} %reshape.143), channel_id=1, replica_groups=mesh['py'=4,'pz'=8] {'py'}, dimensions={0} | all-to-all | bytes 4194304 | tf_op jit(solution)/shard_map/while/body/eval_jaxpr/all_to_all | solution.py:54
  356.8 7.7 %reduce.4 = f32[4,131072]{1,0:T(4,128)S(1)} reduce(f32[4,1,131072]{2,1,0:T(1,128)} %all_to_all.204, f32[]{:T(128)} %broadcast.656), dimensions={1}, to_apply=%all_to_all.178.reduce_sub_computation | reduce | bytes 4194308 | tf_op jit(solution)/shard_map/while/body/eval_jaxpr/all_to_all | solution.py:54
  364.5 6.1 reshape.144
  385.6 46.7 %all-to-all-done.1 = f32[2,16,128,128]{2,1,0,3:T(8,128)S(1)} async-done(((f32[2,16,128,128]{2,1,0,3:T(8,128)}), f32[2,16,128,128]{2,1,0,3:T(8,128)S(1)}, u32[]{:S(2)}, u32[]{:S(2)}) %all-to-all-start.1) | async-done | bytes 2097184 | tf_op jit(solution)/shard_map/while/body/eval_jaxpr/all_to_all | solution.py:53
  467.6 28.1 %all_to_all.205 = f32[2,128,128,16]{1,3,0,2:T(8,128)S(1)} all-to-all(f32[2,128,128,16]{1,3,0,2:T(8,128)S(1)} %copy.151), channel_id=1, replica_groups=mesh['py'=4,'pz'=8] {'py'}, dimensions={2} | all-to-all | bytes 4194304 | tf_op jit(solution)/shard_map/while/body/eval_jaxpr/all_to_all | solution.py:71
  500.5 7.2 %reshape.145 = f32[8,1,65536]{2,1,0:T(1,128)} reshape(f32[128,2,32,64]{3,2,1,0:T(8,128)} %bitcast.327) | data formatting | bytes 4194304 | tf_op jit(solution)/shard_map/while
  511.6 48.0 %all-to-all-done.3 = f32[8,1,65536]{2,1,0:T(1,128)S(1)} async-done(((f32[8,1,65536]{2,1,0:T(1,128)}), f32[8,1,65536]{2,1,0:T(1,128)S(1)}, u32[]{:S(2)}, u32[]{:S(2)}) %all-to-all-start.3) | async-done | bytes 2097184 | tf_op jit(solution)/shard_map/while/body/eval_jaxpr/all_to_all | solution.py:70
  561.5 7.2 %reduce.5 = f32[8,65536]{1,0:T(8,128)S(1)} reduce(f32[8,1,65536]{2,1,0:T(1,128)} %copy-done, f32[]{:T(128)} %broadcast.657), dimensions={1}, to_apply=%all_to_all.189.reduce_sub_computation | reduce | bytes 4194308 | tf_op jit(solution)/shard_map/while/body/eval_jaxpr/all_to_all | solution.py:70
  572.3 7.0 %copy.154 = f32[2,16,32,8,64]{2,4,3,1,0:T(8,128)} copy(f32[2,16,32,8,64]{4,2,0,1,3:T(8,128)} %bitcast.326) | data formatting | bytes 4194304 | tf_op jit(solution)/shard_map/while/body/eval_jaxpr/all_to_all | solution.py:70
  579.3 7.9 %copy.155 = f32[2,16,32,4,8,16]{2,5,4,3,1,0:T(8,128)} copy(f32[2,16,32,4,8,16]{2,5,3,4,1,0:T(8,128)} %bitcast.320) | data formatting | bytes 4194304 | tf_op jit(solution)/shard_map/while/body/eval_jaxpr/transpose | solution.py:78
  587.2 5.6 copy.156
  603.1 6.5 multiply_reduce_fusion.1
  609.6 37.5 %all-reduce = (f32[8]{0:T(128)S(1)}, f32[8]{0:T(128)S(1)}) all-reduce(f32[8]{0:T(128)S(1)} %get-tuple-element.349, f32[8]{0:T(128)S(1)} %get-tuple-element.348), channel_id=1, replica_groups=mesh['py'=4,'pz'=8] {'py','pz'}, use_global_device_ids=true, to_apply=%region_3.4 | all-reduce | flops 16 | bytes 128 | tf_op jit(solution)/shard_map/psum | solution.py:101
  651.4 41.5 %psum.23 = f32[8]{0:T(128)S(1)} all-reduce(f32[8]{0:T(128)S(1)} %multiply_reduce_fusion), channel_id=1, replica_groups=mesh['py'=4,'pz'=8] {'py','pz'}, use_global_device_ids=true, to_apply=%region_7.8 | all-reduce | flops 8 | bytes 64 | tf_op jit(solution)/shard_map/psum | solution.py:104
  (122 shorter events, 162.0 us)
Async XLA Ops:
  3.2 599.9 %copy-start.4 = (f32[16,32,128]{2,1,0:T(8,128)S(1)}, f32[16,32,128]{2,1,0:T(8,128)}, u32[]{:S(2)}) copy-start(f32[16,32,128]{2,1,0:T(8,128)} %param.7) | copy-start | bytes 786436
  81.3 54.2 %all-to-all-start.1 = ((f32[2,16,128,128]{2,1,0,3:T(8,128)}), f32[2,16,128,128]{2,1,0,3:T(8,128)S(1)}, u32[]{:S(2)}, u32[]{:S(2)}) async-start(f32[2,16,128,128]{2,1,0,3:T(8,128)} %copy.145), calls=%async_computation.1 | async-start | bytes 4194304 | tf_op jit(solution)/shard_map/while/body/eval_jaxpr/all_to_all | solution.py:53
  138.5 3.5 copy-start.1
  211.0 51.9 %all-to-all-start.3 = ((f32[8,1,65536]{2,1,0:T(1,128)}), f32[8,1,65536]{2,1,0:T(1,128)S(1)}, u32[]{:S(2)}, u32[]{:S(2)}) async-start(f32[8,1,65536]{2,1,0:T(1,128)} %reshape.145), calls=%async_computation.3 | async-start | bytes 4194304 | tf_op jit(solution)/shard_map/while/body/eval_jaxpr/all_to_all | solution.py:70
  262.9 1.4 copy-start
  298.6 2.5 copy-start.2
  301.3 2.0 copy-start.3
  380.5 51.7 %all-to-all-start.1 = ((f32[2,16,128,128]{2,1,0,3:T(8,128)}), f32[2,16,128,128]{2,1,0,3:T(8,128)S(1)}, u32[]{:S(2)}, u32[]{:S(2)}) async-start(f32[2,16,128,128]{2,1,0,3:T(8,128)} %copy.145), calls=%async_computation.1 | async-start | bytes 4194304 | tf_op jit(solution)/shard_map/while/body/eval_jaxpr/all_to_all | solution.py:53
  435.2 3.5 copy-start.1
  507.7 51.9 %all-to-all-start.3 = ((f32[8,1,65536]{2,1,0:T(1,128)}), f32[8,1,65536]{2,1,0:T(1,128)S(1)}, u32[]{:S(2)}, u32[]{:S(2)}) async-start(f32[8,1,65536]{2,1,0:T(1,128)} %reshape.145), calls=%async_computation.3 | async-start | bytes 4194304 | tf_op jit(solution)/shard_map/while/body/eval_jaxpr/all_to_all | solution.py:70
  559.6 1.4 copy-start
  595.2 2.5 copy-start.2
  598.0 2.0 copy-start.3
  647.1 4.2 copy-start.5
  647.2 45.7 %copy-start.6 = (s32[8]{0:T(128)S(1)}, s32[8]{0:T(128)}, u32[]{:S(2)}) copy-start(s32[8]{0:T(128)} %param.9) | copy-start | bytes 100
where the time goes:
time: 697 us; the launch traced here: 694 us
  blocking collectives  195 us (28%)
  waiting for transfers between devices  189 us (27%)
  local copies, waits for them, and re-layouts  156 us (22%)
  matrix products  85.4 us (12%)
  other arithmetic  44.8 us (6%)
  starting transfers between devices  18.7 us (3%)
    all_to_all x2, waiting for transfers between devices, slab_kinetic(): lax.all_to_all(lax.all_to_all(spatial, 'py', split_axis=2, concat_axis=3,...  96 us
    all_to_all x2, waiting for transfers between devices, slab_kinetic(): lax.all_to_all(lax.all_to_all(flat, 'py', split_axis=3, concat_axis=2, ti...  92.9 us
    all_to_all x2, blocking collectives, slab_kinetic(): lax.all_to_all(flat, 'py', split_axis=3, concat_axis=2, tiled=True)  59.3 us
    all_to_all x2, blocking collectives, slab_kinetic(): lax.all_to_all(spatial, 'py', split_axis=2, concat_axis=3, tiled=True)  56.3 us
    while x24, local copies, waits for them, and re-layouts  52.9 us
    psum x1, blocking collectives, body(): lax.psum(jnp.sum(residual * residual, axis=(0, 2, 3, 4)), ('py', 'pz'))  41.5 us
    psum x1, blocking collectives, body(): lax.psum((norm_local, correlation_local), ('py', 'pz'))  37.5 us
    dot_general x12, matrix products, transform_axis(): jnp.einsum(form, imag_part, sines, precision=high)  22.5 us
  transfers between devices with their start and end apart: 4, of which 4 were waited for; matrix products, arithmetic and copies ran while one was open for 0% of the time, Pallas kernels for 0%

commit v1 on v0

--- a/solution.py
+++ b/solution.py
@@ -51,7 +51,10 @@
     along_x = transform_axis(field, 4, forward)
     flat = jnp.moveaxis(along_x, 1, 3).reshape(parts, rows_z, rows_y, bands * length)
     planes = lax.all_to_all(
-        lax.all_to_all(flat, "py", split_axis=3, concat_axis=2, tiled=True),
+        jnp.concatenate(
+            lax.all_to_all(jnp.stack(jnp.split(flat, lax.axis_size("py"), axis=3)), "py", 0, 0),
+            axis=2,
+        ),
         "pz",
         split_axis=3,
         concat_axis=1,

time: 697 us -> 625 us (0.90)
  local copies, waits for them, and re-layouts: 156 us -> 101 us
  other arithmetic: 44.8 us -> 29.9 us
    while x24 -> x20, local copies, waits for them, and re-layouts: 52.9 us -> 28.4 us
    all_to_all x10 -> x2, local copies, waits for them, and re-layouts: 23.3 us -> 2.43 us  [slab_kinetic(): lax.all_to_all(jnp.concatenate(lax.all_to_all(jnp.stack(jnp.split(flat, l...]
    all_to_all x2 -> x0, other arithmetic: 15.4 us -> none  [slab_kinetic(): lax.all_to_all(flat, 'py', split_axis=3, concat_axis=2, tiled=True)]
    reshape x2 -> x4, local copies, waits for them, and re-layouts: 15 us -> 4.54 us  [slab_kinetic(): jnp.concatenate(lax.all_to_all(jnp.stack(jnp.split(flat, lax.axis_size('p...]
where the time goes in v1:
time: 625 us; the launch traced here: 622 us
  blocking collectives  193 us (31%)
  waiting for transfers between devices  189 us (30%)
  local copies, waits for them, and re-layouts  101 us (16%)
  matrix products  85.5 us (14%)
  other arithmetic  29.9 us (5%)
  starting transfers between devices  17.8 us (3%)
    all_to_all x2, waiting for transfers between devices, slab_kinetic(): lax.all_to_all(lax.all_to_all(spatial, 'py', split_axis=2, concat_axis=3,...  96 us
    all_to_all x2, waiting for transfers between devices, slab_kinetic(): lax.all_to_all(jnp.concatenate(lax.all_to_all(jnp.stack(jnp.split(flat, l...  93.3 us
    all_to_all x2, blocking collectives, slab_kinetic(): lax.all_to_all(jnp.stack(jnp.split(flat, lax.axis_size('py'), axis=3)), '...  57.9 us
    all_to_all x2, blocking collectives, slab_kinetic(): lax.all_to_all(spatial, 'py', split_axis=2, concat_axis=3, tiled=True)  56.3 us
    psum x1, blocking collectives, body(): lax.psum(jnp.sum(residual * residual, axis=(0, 2, 3, 4)), ('py', 'pz'))  41.5 us
    psum x1, blocking collectives, body(): lax.psum((norm_local, correlation_local), ('py', 'pz'))  37.5 us
    while x20, local copies, waits for them, and re-layouts  28.4 us
    dot_general x12, matrix products, transform_axis(): jnp.einsum(form, imag_part, sines, precision=high)  22.5 us
  transfers between devices with their start and end apart: 4, of which 4 were waited for; matrix products, arithmetic and copies ran while one was open for 0% of the time, Pallas kernels for 0%

profile of v1, /device:TPU:0, one launch (start us, length us, event | category | flops | bytes accessed | tf_op | source)
XLA Modules:
  0.0 621.8 jit_solution(10258507837565134379)
XLA Ops:
  0.6 2.5 broadcast_in_dim.14
  3.2 527.9 %while.18 = (s32[]{:T(128)}, f32[2,8,16,32,128]{4,3,2,1,0:T(8,128)}, f32[2,8,16,32,128]{4,3,2,1,0:T(8,128)}, s32[1]{0:T(128)}, s32[]{:T(128)}, /*index=5*/s32[]{...) while((s32[]{:T(128)}, ...), condition=%wide.region_1.2_spmd.clone.clone, body=%wide.region_0.1_spmd.clone.clone.sunk | while | flops 9678143488 | bytes 220333664 | solution.py:100
  13.8 29.7 %all_to_all.164 = f32[4,2,16,32,128]{4,3,2,1,0:T(8,128)S(1)} all-to-all(f32[4,2,16,32,128]{4,3,2,1,0:T(8,128)S(1)} %pad_maximum_fusion.4), channel_id=1, replica_groups=mesh['py'=4,'pz'=8] {'py'}, dimensions={0} | all-to-all | bytes 4194304 | tf_op jit(solution)/shard_map/while/body/eval_jaxpr/all_to_all | solution.py:55
  45.9 6.2 %all-to-all-start.1 = ((f32[2,16,128,128]{2,1,0,3:T(8,128)}), f32[2,16,128,128]{2,1,0,3:T(8,128)S(1)}, u32[]{:S(2)}, u32[]{:S(2)}) async-start(f32[2,16,128,128]{2,1,0,3:T(8,128)} %copy.140), calls=%async_computation.1 | async-start | bytes 4194304 | tf_op jit(solution)/shard_map/while/body/eval_jaxpr/all_to_all | solution.py:53
  53.1 46.4 %all-to-all-done.1 = f32[2,16,128,128]{2,1,0,3:T(8,128)S(1)} async-done(((f32[2,16,128,128]{2,1,0,3:T(8,128)}), f32[2,16,128,128]{2,1,0,3:T(8,128)S(1)}, u32[]{:S(2)}, u32[]{:S(2)}) %all-to-all-start.1) | async-done | bytes 2097184 | tf_op jit(solution)/shard_map/while/body/eval_jaxpr/all_to_all | solution.py:53
  134.9 28.1 %all_to_all.165 = f32[2,128,128,16]{1,3,0,2:T(8,128)S(1)} all-to-all(f32[2,128,128,16]{1,3,0,2:T(8,128)S(1)} %copy.146), channel_id=1, replica_groups=mesh['py'=4,'pz'=8] {'py'}, dimensions={2} | all-to-all | bytes 4194304 | tf_op jit(solution)/shard_map/while/body/eval_jaxpr/all_to_all | solution.py:74
  163.3 4.5 copy.148
  167.8 7.2 %reshape.165 = f32[8,1,65536]{2,1,0:T(1,128)} reshape(f32[128,2,32,64]{3,2,1,0:T(8,128)} %bitcast.329) | data formatting | bytes 4194304 | tf_op jit(solution)/shard_map/while
  175.0 3.9 all-to-all-start.3
  178.9 48.0 %all-to-all-done.3 = f32[8,1,65536]{2,1,0:T(1,128)S(1)} async-done(((f32[8,1,65536]{2,1,0:T(1,128)}), f32[8,1,65536]{2,1,0:T(1,128)S(1)}, u32[]{:S(2)}, u32[]{:S(2)}) %all-to-all-start.3) | async-done | bytes 2097184 | tf_op jit(solution)/shard_map/while/body/eval_jaxpr/all_to_all | solution.py:73
  228.8 7.2 %reduce.2 = f32[8,65536]{1,0:T(8,128)S(1)} reduce(f32[8,1,65536]{2,1,0:T(1,128)} %copy-done, f32[]{:T(128)} %broadcast.654), dimensions={1}, to_apply=%all_to_all.149.reduce_sub_computation | reduce | bytes 4194308 | tf_op jit(solution)/shard_map/while/body/eval_jaxpr/all_to_all | solution.py:73
  236.0 3.6 reshape.166
  239.6 7.0 %copy.149 = f32[2,16,32,8,64]{2,4,3,1,0:T(8,128)} copy(f32[2,16,32,8,64]{4,2,0,1,3:T(8,128)} %bitcast.328) | data formatting | bytes 4194304 | tf_op jit(solution)/shard_map/while/body/eval_jaxpr/all_to_all | solution.py:73
  246.6 7.9 %copy.150 = f32[2,16,32,4,8,16]{2,5,4,3,1,0:T(8,128)} copy(f32[2,16,32,4,8,16]{2,5,3,4,1,0:T(8,128)} %bitcast.322) | data formatting | bytes 4194304 | tf_op jit(solution)/shard_map/while/body/eval_jaxpr/transpose | solution.py:81
  254.5 5.6 copy.151
  278.1 28.1 %all_to_all.164 = f32[4,2,16,32,128]{4,3,2,1,0:T(8,128)S(1)} all-to-all(f32[4,2,16,32,128]{4,3,2,1,0:T(8,128)S(1)} %pad_maximum_fusion.4), channel_id=1, replica_groups=mesh['py'=4,'pz'=8] {'py'}, dimensions={0} | all-to-all | bytes 4194304 | tf_op jit(solution)/shard_map/while/body/eval_jaxpr/all_to_all | solution.py:55
  308.5 3.8 all-to-all-start.1
  313.3 46.8 %all-to-all-done.1 = f32[2,16,128,128]{2,1,0,3:T(8,128)S(1)} async-done(((f32[2,16,128,128]{2,1,0,3:T(8,128)}), f32[2,16,128,128]{2,1,0,3:T(8,128)S(1)}, u32[]{:S(2)}, u32[]{:S(2)}) %all-to-all-start.1) | async-done | bytes 2097184 | tf_op jit(solution)/shard_map/while/body/eval_jaxpr/all_to_all | solution.py:53
  395.7 28.1 %all_to_all.165 = f32[2,128,128,16]{1,3,0,2:T(8,128)S(1)} all-to-all(f32[2,128,128,16]{1,3,0,2:T(8,128)S(1)} %copy.146), channel_id=1, replica_groups=mesh['py'=4,'pz'=8] {'py'}, dimensions={2} | all-to-all | bytes 4194304 | tf_op jit(solution)/shard_map/while/body/eval_jaxpr/all_to_all | solution.py:74
  424.1 4.5 copy.148
  428.6 7.2 %reshape.165 = f32[8,1,65536]{2,1,0:T(1,128)} reshape(f32[128,2,32,64]{3,2,1,0:T(8,128)} %bitcast.329) | data formatting | bytes 4194304 | tf_op jit(solution)/shard_map/while
  435.8 3.9 all-to-all-start.3
  439.7 48.0 %all-to-all-done.3 = f32[8,1,65536]{2,1,0:T(1,128)S(1)} async-done(((f32[8,1,65536]{2,1,0:T(1,128)}), f32[8,1,65536]{2,1,0:T(1,128)S(1)}, u32[]{:S(2)}, u32[]{:S(2)}) %all-to-all-start.3) | async-done | bytes 2097184 | tf_op jit(solution)/shard_map/while/body/eval_jaxpr/all_to_all | solution.py:73
  489.6 7.2 %reduce.2 = f32[8,65536]{1,0:T(8,128)S(1)} reduce(f32[8,1,65536]{2,1,0:T(1,128)} %copy-done, f32[]{:T(128)} %broadcast.654), dimensions={1}, to_apply=%all_to_all.149.reduce_sub_computation | reduce | bytes 4194308 | tf_op jit(solution)/shard_map/while/body/eval_jaxpr/all_to_all | solution.py:73
  496.8 3.6 reshape.166
  500.4 7.0 %copy.149 = f32[2,16,32,8,64]{2,4,3,1,0:T(8,128)} copy(f32[2,16,32,8,64]{4,2,0,1,3:T(8,128)} %bitcast.328) | data formatting | bytes 4194304 | tf_op jit(solution)/shard_map/while/body/eval_jaxpr/all_to_all | solution.py:73
  507.4 7.9 %copy.150 = f32[2,16,32,4,8,16]{2,5,4,3,1,0:T(8,128)} copy(f32[2,16,32,4,8,16]{2,5,3,4,1,0:T(8,128)} %bitcast.322) | data formatting | bytes 4194304 | tf_op jit(solution)/shard_map/while/body/eval_jaxpr/transpose | solution.py:81
  515.3 5.4 copy.151
  531.1 6.5 %multiply_reduce_fusion.1 = (f32[8]{0:T(128)S(1)}, f32[8]{0:T(128)S(1)}, f32[2,8,16,32,128]{4,3,2,1,0:T(8,128)}) fusion(f32[2,8,16,32,128]{4,3,2,1,0:T(8,128)} %get-tuple-element.450, f32[2,8,16,32,128]{4,3,2,1,0:T(8,128)} %get-tuple-element.289, f32[16,32,128]{2,1,0:T(8,128)S(1)} %copy-done.4), kind=kLoop, calls=%fused_computation.243 | loop fusion | flops 6291440 | bytes 12845120 | tf_op jit(solution)/shard_map/reduce_sum | solution.py:102
  537.6 37.5 %all-reduce = (f32[8]{0:T(128)S(1)}, f32[8]{0:T(128)S(1)}) all-reduce(f32[8]{0:T(128)S(1)} %get-tuple-element.349, f32[8]{0:T(128)S(1)} %get-tuple-element.348), channel_id=1, replica_groups=mesh['py'=4,'pz'=8] {'py','pz'}, use_global_device_ids=true, to_apply=%region_3.4 | all-reduce | flops 16 | bytes 128 | tf_op jit(solution)/shard_map/psum | solution.py:104
  575.2 4.2 multiply_reduce_fusion
  579.4 41.5 %psum.23 = f32[8]{0:T(128)S(1)} all-reduce(f32[8]{0:T(128)S(1)} %multiply_reduce_fusion), channel_id=1, replica_groups=mesh['py'=4,'pz'=8] {'py','pz'}, use_global_device_ids=true, to_apply=%region_7.8 | all-reduce | flops 8 | bytes 64 | tf_op jit(solution)/shard_map/psum | solution.py:107
  (114 shorter events, 117.3 us)
Async XLA Ops:
  3.2 527.9 %copy-start.4 = (f32[16,32,128]{2,1,0:T(8,128)S(1)}, f32[16,32,128]{2,1,0:T(8,128)}, u32[]{:S(2)}) copy-start(f32[16,32,128]{2,1,0:T(8,128)} %param.7) | copy-start | bytes 786436
  45.9 53.7 %all-to-all-start.1 = ((f32[2,16,128,128]{2,1,0,3:T(8,128)}), f32[2,16,128,128]{2,1,0,3:T(8,128)S(1)}, u32[]{:S(2)}, u32[]{:S(2)}) async-start(f32[2,16,128,128]{2,1,0,3:T(8,128)} %copy.140), calls=%async_computation.1 | async-start | bytes 4194304 | tf_op jit(solution)/shard_map/while/body/eval_jaxpr/all_to_all | solution.py:53
  102.5 3.5 copy-start.1
  175.0 51.9 %all-to-all-start.3 = ((f32[8,1,65536]{2,1,0:T(1,128)}), f32[8,1,65536]{2,1,0:T(1,128)S(1)}, u32[]{:S(2)}, u32[]{:S(2)}) async-start(f32[8,1,65536]{2,1,0:T(1,128)} %reshape.165), calls=%async_computation.3 | async-start | bytes 4194304 | tf_op jit(solution)/shard_map/while/body/eval_jaxpr/all_to_all | solution.py:73
  226.9 1.4 copy-start
  262.5 2.5 copy-start.2
  265.3 2.0 copy-start.3
  308.5 51.7 %all-to-all-start.1 = ((f32[2,16,128,128]{2,1,0,3:T(8,128)}), f32[2,16,128,128]{2,1,0,3:T(8,128)S(1)}, u32[]{:S(2)}, u32[]{:S(2)}) async-start(f32[2,16,128,128]{2,1,0,3:T(8,128)} %copy.140), calls=%async_computation.1 | async-start | bytes 4194304 | tf_op jit(solution)/shard_map/while/body/eval_jaxpr/all_to_all | solution.py:53
  363.1 3.5 copy-start.1
  435.8 51.9 %all-to-all-start.3 = ((f32[8,1,65536]{2,1,0:T(1,128)}), f32[8,1,65536]{2,1,0:T(1,128)S(1)}, u32[]{:S(2)}, u32[]{:S(2)}) async-start(f32[8,1,65536]{2,1,0:T(1,128)} %reshape.165), calls=%async_computation.3 | async-start | bytes 4194304 | tf_op jit(solution)/shard_map/while/body/eval_jaxpr/all_to_all | solution.py:73
  487.7 1.4 copy-start
  523.1 2.5 copy-start.2
  525.9 2.0 copy-start.3
  575.2 4.2 copy-start.5
  575.2 45.7 %copy-start.6 = (s32[8]{0:T(128)S(1)}, s32[8]{0:T(128)}, u32[]{:S(2)}) copy-start(s32[8]{0:T(128)} %param.9) | copy-start | bytes 100
